TPU v7x, 256 devices: a whole 4x4x8 slice. The times are simulated.
256 devices in a mesh: batch: 2 (over core), neuron: 128 (over z, y, x).
Axes of the slice: x: 4, y: 4, z: 8, core: 2. Of those that a mesh axis runs over, the one named last changes fastest.
Arguments:
- images: bfloat16 [32, 65536], P('batch', 'neuron'), parts along dimension 0, may hold values from 0 to 32
- tile_weights: bfloat16 [2, 16384, 128, 128], P(None, 'neuron'), may hold values from -0.375 to 0.375
- tile_blocks: int32 [2, 16384, 2], P(None, 'neuron'), may hold values from 0 to 511, as said below
- tile_count: int32 [2, 128], P(None, 'neuron'), may hold values from 96 to 128, as said below
- bias: float32 [2, 65536], P(None, 'neuron'), may hold values from -48 to 48
Outputs:
- activity: bfloat16 [32, 65536], P('batch', 'neuron'), parts along dimension 0
There are 2 independent parts, one for each index of `batch`. A program takes and returns all parts, laid end to end along the dimension named above; an argument that names none is the same for every part. Nothing has to cross between parts.
Inputs may be any that keep to these rules, and one draw needn't show every extreme that they name: Slots 0 to tile_count[l, d] - 1 of device d are live in layer l; in every layer one device has all 128 live. `tile_blocks`: entry [l, d * 128 + s, :] is the row block and column block of slot s of device d. Within one device and layer the column blocks are all different, and at most 2 of them lie among the 4 column blocks of any one neuron device; in every layer the column blocks of some neuron device get exactly 2 live slots from every device.
All inputs are finite; a program needn't handle non-finite values.
Results may differ from a plain program's by a relative error of at most 0.0033.
Values may be sent and summed in bfloat16 or wider, within the bound.
A program may use at most 64 MiB of HBM per device.

v0:
```python
import jax
import jax.numpy as jnp
from jax import lax
from jax.sharding import Mesh
from jax.sharding import PartitionSpec as P

NEURON = ("neuron_0", "neuron_1", "neuron_2")


CEILING = 32.0


def gathered_by_axis(value, axes, dim):
    if not axes:
        return value
    nearer = lax.all_gather(value, axes[-1], axis=dim, tiled=True)
    return gathered_by_axis(nearer, axes[:-1], dim)


def local(images, tile_weights, tile_blocks, tile_count, bias):
    devices = lax.axis_size(NEURON)
    layer_total = tile_weights.shape[0]
    slot_total = tile_weights.shape[1]
    block_width = tile_weights.shape[2]
    image_rows, local_width = images.shape
    own_blocks = local_width // block_width
    all_blocks = own_blocks * devices
    capacity = max(2, slot_total // devices)
    slot_ids = jnp.arange(slot_total, dtype=jnp.int32)
    activity = images
    for layer_index in range(layer_total):
        whole_acts = gathered_by_axis(activity, NEURON, 1)
        block_view = whole_acts.reshape(image_rows, all_blocks, block_width)
        row_ids = tile_blocks[layer_index, :, 0]
        col_ids = tile_blocks[layer_index, :, 1]
        usable = slot_ids < tile_count[layer_index, 0]
        picked = jnp.take(block_view, row_ids, axis=1)
        products = jnp.einsum(
            "bsk,skn->sbn", picked, tile_weights[layer_index], preferred_element_type=jnp.float32
        )
        products = jnp.where(usable[:, None, None], products, 0.0)
        owners = col_ids // own_blocks
        local_block = (col_ids % own_blocks).astype(jnp.float32)
        same_owner = (
            (owners[:, None] == owners[None, :])
            & usable[None, :]
            & (slot_ids[None, :] < slot_ids[:, None])
        )
        slot_rank = jnp.sum(same_owner.astype(jnp.int32), axis=1)
        targets = jnp.where(usable, owners * capacity + slot_rank, devices * capacity)
        outgoing = (
            jnp.zeros((devices * capacity, image_rows, block_width), jnp.float32)
            .at[targets]
            .set(products, mode="drop")
        )
        labels = (
            jnp.full((devices * capacity,), -1.0, jnp.float32)
            .at[targets]
            .set(local_block, mode="drop")
        )
        incoming, arrived_ids = (
            lax.all_to_all(outgoing, NEURON, split_axis=0, concat_axis=0, tiled=True),
            lax.all_to_all(labels, NEURON, split_axis=0, concat_axis=0, tiled=True),
        )
        selector = (
            arrived_ids[None, :] == jnp.arange(own_blocks, dtype=jnp.float32)[:, None]
        ).astype(jnp.float32)
        summed = jnp.einsum("or,rbn->obn", selector, incoming, precision=lax.Precision.HIGHEST)
        summed = jnp.transpose(summed, (1, 0, 2)).reshape(image_rows, local_width)
        activity = jnp.clip(summed + bias[layer_index][None, :], 0.0, CEILING).astype(jnp.bfloat16)
    return activity


def solution(mesh):
    split = Mesh(
        mesh.devices.reshape(mesh.shape["batch"], 8, 4, 4),
        ("batch", "neuron_0", "neuron_1", "neuron_2"),
    )
    in_specs = (
        P("batch", NEURON),
        P(None, NEURON, None, None),
        P(None, NEURON, None),
        P(None, NEURON),
        P(None, NEURON),
    )
    out_specs = P("batch", NEURON)
    return jax.shard_map(local, mesh=split, in_specs=in_specs, out_specs=out_specs, check_vma=False)
```

profile of v0, /device:TPU:32, one launch (start us, length us, event | category | flops | bytes accessed | tf_op | source)
XLA Modules:
  0.0 308.1 jit_solution(2130739490381186020)
XLA Ops:
  6.5 12.4 %all_gather.18 = bf16[16,2048]{1,0:T(8,128)(2,1)S(1)} all-gather(bf16[16,512]{1,0:T(8,128)(2,1)} %param.7), channel_id=1, replica_groups=mesh['batch'=2,'neuron_0'=8,'neuron_1'=4,'neuron_2'=4] {'neuron_2'}, dimensions={1}, use_global_device_ids=true | all-gather | bytes 81920 | tf_op jit(solution)/shard_map/all_gather | solution.py:16
  18.9 13.5 %all_gather.19 = bf16[16,8192]{1,0:T(8,128)(2,1)} all-gather(bf16[16,2048]{1,0:T(8,128)(2,1)S(1)} %all_gather.18), channel_id=1, replica_groups=mesh['batch'=2,'neuron_0'=8,'neuron_1'=4,'neuron_2'=4] {'neuron_1'}, dimensions={1}, use_global_device_ids=true | all-gather | bytes 327680 | tf_op jit(solution)/shard_map/all_gather | solution.py:16
  32.5 0.0 all-gather.3.cloned.1.call-update
  32.5 1.3 fusion.47
  33.8 0.6 iota_compare_fusion.3
  34.4 0.6 iota_compare_fusion.4
  35.0 0.7 fusion.37
  35.7 0.7 fusion.36
  36.4 0.7 and_select_fusion.4
  37.1 0.2 convert_reduce_fusion
  37.3 1.9 fusion.43
  39.2 1.0 scatter_custom_fusion.1
  40.2 0.8 all_to_all.20
  41.0 13.7 %all-to-all-start.1 = ((f32[128,2,1]{1,2,0:T(1,128)}), f32[128,2,1]{1,2,0:T(1,128)S(1)}, u32[]{:S(2)}, u32[]{:S(2)}) async-start(f32[128,2,1]{1,2,0:T(1,128)} %bitcast.13), calls=%async_computation.1 | async-start | bytes 131072 | tf_op jit(solution)/shard_map/all_to_all | solution.py:63
  54.7 0.7 compare_and_fusion
  55.4 19.4 %all-gather.3.cloned.1.call-done = bf16[16,65536]{1,0:T(8,128)(2,1)} async-done(((bf16[16,8192]{1,0:T(8,128)(2,1)}), bf16[16,65536]{1,0:T(8,128)(2,1)}) %all-gather.3.cloned.1.call-update) | async-done | bytes 2097168 | tf_op jit(solution)/shard_map/all_gather | solution.py:16
  74.7 2.0 copy_bitcast_fusion.1
  76.7 0.7 gather_fusion
  77.4 3.2 %fusion.10 = f32[128,16,128]{2,1,0:T(8,128)S(1)} fusion(bf16[2,128,128,128]{3,2,1,0:T(8,128)(2,1)} %param.8, bf16[128,16,128]{2,1,0:T(8,128)(2,1)S(1)} %gather_fusion, pred[128]{0:T(512)(128)(4,1)S(1)} %get-tuple-element.16, pred[128]{0:T(512)(128)(4,1)S(1)} %iota_compare_fusion.3), kind=kOutput, calls=%fused_computation.18 | convolution fusion | flops 67633152 | bytes 5767424 | tf_op jit(solution)/shard_map/bsk,skn->sbn/dot_general | solution.py:38
  80.6 1.5 broadcast.296.clone
  82.1 13.7 %scatter_fusion = f32[256,16,128]{2,1,0:T(8,128)} fusion(f32[256,16,128]{2,1,0:T(8,128)} %broadcast.296.clone, s32[128]{0:T(128)S(1)} %get-tuple-element.18, f32[128,16,128]{2,1,0:T(8,128)S(1)} %fusion.10), kind=kCustom, calls=%fused_computation.4 | custom fusion | bytes 3146240 | tf_op jit(solution)/shard_map/scatter | solution.py:54
  95.7 0.0 all-to-all-done.1
  95.7 11.6 %all-to-all-start.2 = ((f32[256,16,128]{2,1,0:T(8,128)}), f32[256,16,128]{2,1,0:T(8,128)S(1)}, u32[]{:S(2)}, u32[]{:S(2)}) async-start(f32[256,16,128]{2,1,0:T(8,128)} %scatter_fusion), calls=%async_computation.2 | async-start | bytes 4194304 | tf_op jit(solution)/shard_map/all_to_all | solution.py:62
  107.3 0.0 all-gather.5.cloned.1.call-start
  107.4 0.5 broadcast.363
  107.9 0.8 reduce.6
  108.7 0.1 eq.69
  108.8 47.8 %all-to-all-done.2 = f32[256,16,128]{2,1,0:T(8,128)S(1)} async-done(((f32[256,16,128]{2,1,0:T(8,128)}), f32[256,16,128]{2,1,0:T(8,128)S(1)}, u32[]{:S(2)}, u32[]{:S(2)}) %all-to-all-start.2) | async-done | bytes 2097184 | tf_op jit(solution)/shard_map/all_to_all | solution.py:62
  156.7 1.3 fusion.8
  158.0 11.9 %all_gather.21 = bf16[16,2048]{1,0:T(8,128)(2,1)S(1)} all-gather(bf16[16,512]{1,0:T(8,128)(2,1)S(1)} %fusion.29), channel_id=1, replica_groups=mesh['batch'=2,'neuron_0'=8,'neuron_1'=4,'neuron_2'=4] {'neuron_2'}, dimensions={1}, use_global_device_ids=true | all-gather | bytes 81920 | tf_op jit(solution)/shard_map/all_gather | solution.py:16
  169.9 13.0 %all_gather.22 = bf16[16,8192]{1,0:T(8,128)(2,1)} all-gather(bf16[16,2048]{1,0:T(8,128)(2,1)S(1)} %all_gather.21), channel_id=1, replica_groups=mesh['batch'=2,'neuron_0'=8,'neuron_1'=4,'neuron_2'=4] {'neuron_1'}, dimensions={1}, use_global_device_ids=true | all-gather | bytes 327680 | tf_op jit(solution)/shard_map/all_gather | solution.py:16
  182.9 0.0 all-gather.5.cloned.1.call-update
  182.9 1.0 scatter_custom_fusion
  183.9 0.8 all_to_all.18
  184.6 6.9 %all-to-all-start = ((f32[128,2,1]{1,2,0:T(1,128)}), f32[128,2,1]{1,2,0:T(1,128)S(1)}, u32[]{:S(2)}, u32[]{:S(2)}) async-start(f32[128,2,1]{1,2,0:T(1,128)} %bitcast.5), calls=%async_computation | async-start | bytes 131072 | tf_op jit(solution)/shard_map/all_to_all | solution.py:63
  191.5 26.7 %all-gather.5.cloned.1.call-done = bf16[16,65536]{1,0:T(8,128)(2,1)} async-done(((bf16[16,8192]{1,0:T(8,128)(2,1)}), bf16[16,65536]{1,0:T(8,128)(2,1)}) %all-gather.5.cloned.1.call-update) | async-done | bytes 2097168 | tf_op jit(solution)/shard_map/all_gather | solution.py:16
  218.2 2.0 copy_bitcast_fusion
  220.1 0.7 gather_fusion.1
  220.8 3.2 %fusion.13 = f32[128,16,128]{2,1,0:T(8,128)S(1)} fusion(bf16[2,128,128,128]{3,2,1,0:T(8,128)(2,1)} %param.8, bf16[128,16,128]{2,1,0:T(8,128)(2,1)S(1)} %gather_fusion.1, pred[128]{0:T(512)(128)(4,1)S(1)} %get-tuple-element.8, pred[128]{0:T(512)(128)(4,1)S(1)} %iota_compare_fusion.4), kind=kOutput, calls=%fused_computation.19 | convolution fusion | flops 67633152 | bytes 5767424 | tf_op jit(solution)/shard_map/bsk,skn->sbn/dot_general | solution.py:38
  224.0 1.5 broadcast.296
  225.5 13.5 %scatter_fusion.1 = f32[256,16,128]{2,1,0:T(8,128)} fusion(f32[256,16,128]{2,1,0:T(8,128)} %broadcast.296, s32[128]{0:T(128)S(1)} %get-tuple-element.19, f32[128,16,128]{2,1,0:T(8,128)S(1)} %fusion.13), kind=kCustom, calls=%fused_computation.5 | custom fusion | bytes 3146240 | tf_op jit(solution)/shard_map/scatter | solution.py:54
  239.0 0.0 all-to-all-done
  239.0 12.1 %all-to-all-start.3 = ((f32[256,16,128]{2,1,0:T(8,128)}), f32[256,16,128]{2,1,0:T(8,128)S(1)}, u32[]{:S(2)}, u32[]{:S(2)}) async-start(f32[256,16,128]{2,1,0:T(8,128)} %scatter_fusion.1), calls=%async_computation.3 | async-start | bytes 4194304 | tf_op jit(solution)/shard_map/all_to_all | solution.py:62
  251.1 0.8 reduce.7
  251.9 0.1 eq.62
  252.0 47.2 %all-to-all-done.3 = f32[256,16,128]{2,1,0:T(8,128)S(1)} async-done(((f32[256,16,128]{2,1,0:T(8,128)}), f32[256,16,128]{2,1,0:T(8,128)S(1)}, u32[]{:S(2)}, u32[]{:S(2)}) %all-to-all-start.3) | async-done | bytes 2097184 | tf_op jit(solution)/shard_map/all_to_all | solution.py:62
  299.3 1.3 fusion.6
  300.6 0.6 fusion.27
  (7 shorter events, 0.0 us)
Async XLA Ops:
  6.5 68.2 %all-gather.3.cloned.1.call-start = ((), (), s32[]{:S(2)}) async-start(), calls=%async_computation.4 | async-start | bytes 2359296 | tf_op jit(solution)/shard_map/all_gather | solution.py:16
  41.0 54.7 %all-to-all-start.1 = ((f32[128,2,1]{1,2,0:T(1,128)}), f32[128,2,1]{1,2,0:T(1,128)S(1)}, u32[]{:S(2)}, u32[]{:S(2)}) async-start(f32[128,2,1]{1,2,0:T(1,128)} %bitcast.13), calls=%async_computation.1 | async-start | bytes 131072 | tf_op jit(solution)/shard_map/all_to_all | solution.py:63
  95.7 11.6 %copy-start = (f32[2,512]{1,0:T(2,128)S(1)}, f32[2,512]{1,0:T(2,128)}, u32[]{:S(2)}) copy-start(f32[2,512]{1,0:T(2,128)} %param.11) | copy-start | bytes 12292
  95.7 61.0 %all-to-all-start.2 = ((f32[256,16,128]{2,1,0:T(8,128)}), f32[256,16,128]{2,1,0:T(8,128)S(1)}, u32[]{:S(2)}, u32[]{:S(2)}) async-start(f32[256,16,128]{2,1,0:T(8,128)} %scatter_fusion), calls=%async_computation.2 | async-start | bytes 4194304 | tf_op jit(solution)/shard_map/all_to_all | solution.py:62
  107.3 110.9 %all-gather.5.cloned.1.call-start = ((), (), s32[]{:S(2)}) async-start(), calls=%async_computation.5 | async-start | bytes 2359296 | tf_op jit(solution)/shard_map/all_gather | solution.py:16
  184.6 54.3 %all-to-all-start = ((f32[128,2,1]{1,2,0:T(1,128)}), f32[128,2,1]{1,2,0:T(1,128)S(1)}, u32[]{:S(2)}, u32[]{:S(2)}) async-start(f32[128,2,1]{1,2,0:T(1,128)} %bitcast.5), calls=%async_computation | async-start | bytes 131072 | tf_op jit(solution)/shard_map/all_to_all | solution.py:63
  239.0 60.3 %all-to-all-start.3 = ((f32[256,16,128]{2,1,0:T(8,128)}), f32[256,16,128]{2,1,0:T(8,128)S(1)}, u32[]{:S(2)}, u32[]{:S(2)}) async-start(f32[256,16,128]{2,1,0:T(8,128)} %scatter_fusion.1), calls=%async_computation.3 | async-start | bytes 4194304 | tf_op jit(solution)/shard_map/all_to_all | solution.py:62
Sparse Core Ops, SparseCore 0:
  32.6 42.0 all-gather.2
  183.0 35.1 all-gather.4
where the time goes:
time: 310 us; the launch traced here: 308 us
  waiting for transfers between devices  141 us (45%)
  blocking collectives  50.8 us (16%)
  starting transfers between devices  44.3 us (14%)
  local copies, waits for them, and re-layouts  41 us (13%)
  between operations  13.6 us (4%)
  matrix products  9 us (3%)
  other arithmetic  8.36 us (3%)
    all_to_all x2, waiting for transfers between devices, local(): lax.all_to_all(outgoing, NEURON, split_axis=0, concat_axis=0, tiled=True)  95.1 us
    all_gather x4, blocking collectives, gathered_by_axis(): nearer = lax.all_gather(value, axes[-1], axis=dim, tiled=True)  50.8 us
    all_gather x2, waiting for transfers between devices, gathered_by_axis(): nearer = lax.all_gather(value, axes[-1], axis=dim, tiled=True)  46 us
    scatter x2, local copies, waits for them, and re-layouts, local(): outgoing = jnp.zeros((devices * capacity, image_rows, block_width), jnp.f...  27.1 us
    all_to_all x2, starting transfers between devices, local(): lax.all_to_all(outgoing, NEURON, split_axis=0, concat_axis=0, tiled=True)  23.7 us
    all_to_all x2, starting transfers between devices, local(): lax.all_to_all(labels, NEURON, split_axis=0, concat_axis=0, tiled=True)  20.5 us
    dot_general x2, matrix products, local(): jnp.einsum('bsk,skn->sbn', picked, tile_weights[layer_index], preferred_e...  6.35 us
  transfers between devices with their start and end apart: 6, of which 4 were waited for; matrix products, arithmetic and copies ran while one was open for 17% of the time, Pallas kernels for 0%

commit v1 on v0

v1 whole, which is shorter than its diff:
```python
import functools

import jax
import jax.numpy as jnp
from jax import lax
from jax.experimental import pallas as pl
from jax.experimental.pallas import tpu as pltpu
from jax.sharding import Mesh
from jax.sharding import PartitionSpec as P

AXES = ("neuron_0", "neuron_1", "neuron_2")
Z, Y, X = AXES
CEILING = 32.0
WEIGHT_TOP = 0.375
MESH = pl.DeviceIdType.MESH
LANES = 128


class Part:
    def __init__(self, order, sizes, base, width):
        self.order = order
        self.n1, self.n2, self.n3 = (sizes[a] for a in order)
        self.base = base
        self.width = width

    def start(self, c3, c2, c1):
        return self.base + ((c3 * self.n2 + c2) * self.n1 + c1) * self.width

    def messages(self):
        out = [("a", o) for o in range(1, self.n1)]
        out += [("b", o) for o in range(1, self.n2)]
        half = self.n2 // 2
        for step in range(1, self.n3 // 2 + 1):
            for rel in range(self.n2):
                for way in (1, -1):
                    if 2 * step == self.n3 and (rel < half) != (way == 1):
                        continue
                    out.append(("c", step, rel, way))
        return out


def gather_parts(sizes):
    total = sizes[Z] * sizes[Y] * sizes[X]
    return [
        Part((X, Y, Z), sizes, 0, 2),
        Part((Z, Y, X), sizes, 2 * total, 1),
        Part((Z, X, Y), sizes, 3 * total, 1),
    ]


def encode(value, scale):
    coded = value * lax.rsqrt(jnp.abs(value) + 1e-30) * scale
    return jnp.round(coded).astype(jnp.int32).astype(jnp.int16)


def decode(coded):
    value = coded.astype(jnp.int32).astype(jnp.float32)
    return value * jnp.abs(value)


def kernel(sizes, layers, slots, rows, images, weights, blocks, count, bias, out, *scratch):
    (acts, held, products, table, peer, stab, speer, x_out, x_in, x_out2, x_in2, x_own,
     y_out, y_in, y_out2, y_in2, y_own, z_out, z_in, z_own,
     ag_send, ag_recv, rs_send, rs_recv, tab_send, tab_recv, copy_sem) = scratch
    nz, ny, nx = sizes[Z], sizes[Y], sizes[X]
    me = {axis: lax.axis_index(axis) for axis in AXES}
    zh = nz // 2
    width = rows * 0 + LANES
    shift_x, shift_y = nx.bit_length() - 1, ny.bit_length() - 1
    total = nz * ny * nx
    top = WEIGHT_TOP * CEILING * width
    scale1 = 32700.0 / top ** 0.5
    scale2 = 32700.0 / (top * max(nx, ny)) ** 0.5
    scale3 = 32700.0 / (top * nx * ny) ** 0.5
    back1, back2, back3 = 1 / scale1**2, 1 / scale2**2, 1 / scale3**2

    def other(axis, step):
        return lax.rem(me[axis] + step + sizes[axis], sizes[axis])

    barrier = pltpu.get_barrier_semaphore()
    partners = [(axis, o) for axis in AXES for o in range(1, sizes[axis])]
    for axis, o in partners:
        pl.semaphore_signal(barrier, inc=1, device_id={axis: other(axis, o)}, device_id_type=MESH)

    weight_copies = [
        pltpu.make_async_copy(weights.at[l], held.at[l], copy_sem.at[l]) for l in range(layers)
    ]
    for copy in weight_copies:
        copy.start()

    parts = gather_parts(sizes)

    def own_start(part):
        return part.start(me[part.order[2]], me[part.order[1]], me[part.order[0]])

    def put_acts(layer, j, value):
        if j < 2:
            acts[layer, own_start(parts[0]) + j] = value
        else:
            acts[layer, own_start(parts[j - 1])] = value

    for j in range(4):
        put_acts(0, j, images[:, j * LANES : (j + 1) * LANES])

    lane = lax.broadcasted_iota(jnp.int32, (1, LANES), 1)
    slot = lax.broadcasted_iota(jnp.int32, (LANES, LANES), 0)
    flat = jnp.concatenate(
        [blocks[0], blocks[1], jnp.zeros((4, LANES), jnp.int32)], axis=0
    )
    upright = jnp.transpose(flat)
    dx = lane & (nx - 1)
    dy = (lane >> shift_x) & (ny - 1)
    dz = lane >> (shift_x + shift_y)
    second = jnp.where((dz & 1) == 0, dy, dx)
    place = (second * zh + (dz >> 1)) * 2
    blank = (jnp.where((dz & 1) == 0, ny, nx)) * zh * 2
    for l in range(layers):
        r = blocks[l, 0:1, :]
        j = r & 3
        rx = (r >> 2) & (nx - 1)
        ry = (r >> (2 + shift_x)) & (ny - 1)
        rz = r >> (2 + shift_x + shift_y)
        spot = jnp.where(
            j < 2,
            parts[0].start(rz, ry, rx) + j,
            jnp.where(j == 2, parts[1].start(rx, ry, rz), parts[2].start(ry, rx, rz)),
        )
        table[l : l + 1, :] = spot
        key = jnp.where(slot < count[0, l], slot + 1, 0)
        col = upright[:, 2 * l + 1 : 2 * l + 2]
        before = jnp.zeros((1, LANES), jnp.int32)
        ranked = [jnp.zeros((1, LANES), jnp.int32) for _ in range(2)]
        for j in range(4):
            found = jnp.sum(jnp.where(col == lane * 4 + j, key, 0), axis=0, keepdims=True)
            live = found > 0
            table[8 + 4 * l + j : 9 + 4 * l + j, :] = jnp.where(live, found - 1, slots)
            table[16 + 4 * l + j : 17 + 4 * l + j, :] = jnp.where(live, place + before, blank)
            for k in range(2):
                ranked[k] = ranked[k] + jnp.where(before == k, found, 0)
            before = before + live.astype(jnp.int32)
        for k in range(2):
            table[2 + 2 * l + k : 3 + 2 * l + k, :] = jnp.where(
                ranked[k] > 0, ranked[k] - 1, slots
            )
    own_table = pltpu.make_async_copy(table.at[pl.ds(0, 16)], stab, copy_sem.at[layers])
    own_table.start()

    nothing = jnp.zeros((rows, LANES), jnp.int16)
    products[slots] = nothing
    for buffer in (x_in, y_in):
        for l in range(layers):
            for o in range(buffer.shape[1]):
                buffer[l, o, buffer.shape[2] - 1] = nothing

    pl.semaphore_wait(barrier, len(partners))

    started = []

    def send(src, dst, send_sem, recv_sem, axis, step):
        copy = pltpu.make_async_remote_copy(
            src_ref=src, dst_ref=dst, send_sem=send_sem, recv_sem=recv_sem,
            device_id={axis: other(axis, step)}, device_id_type=MESH,
        )
        copy.start()
        started.append(copy)

    def arrive(dst, send_sem, recv_sem, axis, step):
        pltpu.make_async_remote_copy(
            src_ref=dst, dst_ref=dst, send_sem=send_sem, recv_sem=recv_sem,
            device_id={axis: other(axis, step)}, device_id_type=MESH,
        ).wait_recv()

    def gather(layer):
        number = {}
        for at, part in enumerate(parts):
            for message in part.messages():
                number[(at, message)] = len(number)

        def range_of(part, message, coming):
            a1, a2, a3 = part.order
            kind = message[0]
            if kind == "a":
                first = part.start(me[a3], me[a2], other(a1, -message[1]) if coming else me[a1])
                return first, part.width, a1, message[1]
            if kind == "b":
                first = part.start(me[a3], other(a2, -message[1]) if coming else me[a2], 0)
                return first, part.n1 * part.width, a2, message[1]
            _, step, rel, way = message
            far = step if coming else step - 1
            first = part.start(other(a3, -way * far), other(a2, -rel), 0)
            return first, part.n1 * part.width, a3, way

        def go(at, message):
            n = number.get((at, message))
            if n is None:
                return
            first, size, axis, step = range_of(parts[at], message, False)
            view = acts.at[layer, pl.ds(first, size)]
            send(view, view, ag_send.at[layer, n], ag_recv.at[layer, n], axis, step)

        def come(at, message):
            n = number[(at, message)]
            first, size, axis, step = range_of(parts[at], message, True)
            view = acts.at[layer, pl.ds(first, size)]
            arrive(view, ag_send.at[layer, n], ag_recv.at[layer, n], axis, step)

        order = range(len(parts))
        for at in order:
            for way in (1, -1):
                pass
            for o in range(1, parts[at].n1):
                go(at, ("a", o))
        for at in order:
            for o in range(1, parts[at].n1):
                come(at, ("a", o))
            for way in (1, -1):
                go(at, ("c", 1, 0, way))
            for o in range(1, parts[at].n2):
                go(at, ("b", o))
        for rel in range(1, max(p.n2 for p in parts)):
            for at in order:
                if rel < parts[at].n2:
                    come(at, ("b", rel))
                    for way in (1, -1):
                        go(at, ("c", 1, rel, way))
        for step in range(1, max(p.n3 for p in parts) // 2 + 1):
            for rel in range(max(p.n2 for p in parts)):
                for at in order:
                    for way in (1, -1):
                        if (at, ("c", step, rel, way)) in number:
                            come(at, ("c", step, rel, way))
                            go(at, ("c", step + 1, rel, way))

    sets = [
        (0, X, Y, x_out, x_in, x_out2, x_in2, x_own),
        (1, Y, X, y_out, y_in, y_out2, y_in2, y_own),
    ]
    n_peer = [0, nx - 1]
    for par, a1, a2, *_ in sets:
        for o in range(1, sizes[a1]):
            n = n_peer[par] + o - 1
            send(table.at[pl.ds(16, 8)], peer.at[n], tab_send.at[n], tab_recv.at[n], a1, o)

    def device_of(par, zi, c1, c2):
        y, x = (c2, c1) if par == 0 else (c1, c2)
        return ((2 * zi + par) * ny + y) * nx + x

    def loop(length, body, unroll):
        unroll = min(unroll, length)

        @pl.loop(0, length // unroll)
        def _(at):
            for u in range(unroll):
                body(at * unroll + u)

    for layer in range(layers):
        gather(layer)
        if layer == 0:
            own_table.wait()
            for par, a1, a2, *_ in sets:
                for o in range(1, sizes[a1]):
                    n = n_peer[par] + o - 1
                    arrive(peer.at[n], tab_send.at[n], tab_recv.at[n], a1, o)
            peer_table = pltpu.make_async_copy(peer, speer, copy_sem.at[layers + 1])
            peer_table.start()
        weight_copies[layer].wait()

        def multiply(s):
            got = jnp.dot(
                acts[layer, stab[layer, s]], held[layer, s], preferred_element_type=jnp.float32
            )
            products[s] = encode(got, scale1)

        loop(slots, multiply, 16)
        if layer == 0:
            peer_table.wait()

        sem = 0
        first_sem = {}
        for o in range(1, max(nx, ny)):
            for par, a1, a2, out1, in1, *_ in sets:
                n1, n2 = sizes[a1], sizes[a2]
                if o >= n1:
                    continue
                target = other(a1, o)

                def pack(p):
                    q = p >> 1
                    d = device_of(par, q & (zh - 1), target, q // zh)
                    out1[layer, o - 1, p] = products[stab[2 + 2 * layer + (p & 1), d]]

                loop(n2 * zh * 2, pack, 8)
                first_sem[(par, o)] = sem
                send(
                    out1.at[layer, o - 1], in1.at[layer, o - 1, pl.ds(0, n2 * zh * 2)],
                    rs_send.at[layer, sem], rs_recv.at[layer, sem], a1, o,
                )
                sem += 1

        second_sem = {}
        for par, a1, a2, out1, in1, out2, in2, own in sets:
            n1, n2 = sizes[a1], sizes[a2]
            for o in range(1, n1):
                at = first_sem[(par, o)]
                arrive(
                    in1.at[layer, o - 1, pl.ds(0, n2 * zh * 2)],
                    rs_send.at[layer, at], rs_recv.at[layer, at], a1, o,
                )
            for o2 in list(range(1, n2)) + [0]:
                target = other(a2, o2)

                def add(q):
                    j = q & 3
                    d = device_of(par, q >> 2, me[a1], target)
                    acc = decode(products[stab[8 + 4 * layer + j, d]])
                    for o in range(1, n1):
                        n = n_peer[par] + o - 1
                        acc = acc + decode(in1[layer, o - 1, speer[n, 4 * layer + j, d]])
                    acc = acc * back1
                    if o2:
                        out2[layer, o2 - 1, q] = encode(acc, scale2)
                    else:
                        own[q] = acc

                loop(zh * 4, add, 4)
                if o2:
                    second_sem[(par, o2)] = sem
                    send(
                        out2.at[layer, o2 - 1], in2.at[layer, o2 - 1],
                        rs_send.at[layer, sem], rs_recv.at[layer, sem], a2, o2,
                    )
                    sem += 1

        for par, a1, a2, out1, in1, out2, in2, own in sets:
            n2 = sizes[a2]
            for o in range(1, n2):
                at = second_sem[(par, o)]
                arrive(
                    in2.at[layer, o - 1], rs_send.at[layer, at], rs_recv.at[layer, at], a2, o
                )

            def add(q):
                acc = decode(in2[layer, 0, q])
                for o in range(2, n2):
                    acc = acc + decode(in2[layer, o - 1, q])
                acc = acc * back2 + own[q]
                zt = 2 * (q >> 2) + par
                z_out[layer, zt, q & 3] = encode(acc, scale3)
                z_own[zt, q & 3] = acc

            loop(zh * 4, add, 4)

        third = sem
        for o in range(1, nz):
            send(
                z_out.at[layer, other(Z, o)], z_in.at[layer, o - 1],
                rs_send.at[layer, third + o - 1], rs_recv.at[layer, third + o - 1], Z, o,
            )
        for o in range(1, nz):
            arrive(
                z_in.at[layer, o - 1],
                rs_send.at[layer, third + o - 1], rs_recv.at[layer, third + o - 1], Z, o,
            )
        for j in range(4):
            acc = decode(z_in[layer, 0, j])
            for o in range(2, nz):
                acc = acc + decode(z_in[layer, o - 1, j])
            acc = acc * back3 + z_own[me[Z], j]
            acc = acc + bias[layer : layer + 1, j * LANES : (j + 1) * LANES]
            done = jnp.clip(acc, 0.0, CEILING).astype(jnp.bfloat16)
            if layer + 1 < layers:
                put_acts(layer + 1, j, done)
            else:
                out[:, j * LANES : (j + 1) * LANES] = done

    for copy in started:
        copy.wait_send()


def local(sizes, images, tile_weights, tile_blocks, tile_count, bias):
    layers, slots, width, _ = tile_weights.shape
    rows = images.shape[0]
    nz, ny, nx = sizes[Z], sizes[Y], sizes[X]
    total = nz * ny * nx
    zh = nz // 2
    turned = jnp.transpose(tile_blocks, (0, 2, 1))
    if slots < LANES:
        turned = jnp.pad(turned, ((0, 0), (0, 0), (0, LANES - slots)), constant_values=0)
    counts = jnp.transpose(tile_count, (1, 0))
    block = (rows, LANES)
    n_ag = sum(len(part.messages()) for part in gather_parts(sizes))
    n_rs = 2 * (nx - 1) + 2 * (ny - 1) + nz - 1
    n_peer = nx - 1 + ny - 1

    def half(n1, n2):
        return [
            pltpu.VMEM((layers, n1 - 1, n2 * zh * 2, *block), jnp.int16),
            pltpu.VMEM((layers, n1 - 1, n2 * zh * 2 + 1, *block), jnp.int16),
            pltpu.VMEM((layers, n2 - 1, zh * 4, *block), jnp.int16),
            pltpu.VMEM((layers, n2 - 1, zh * 4, *block), jnp.int16),
            pltpu.VMEM((zh * 4, *block), jnp.float32),
        ]

    scratch = [
        pltpu.VMEM((layers, total * 4, *block), jnp.bfloat16),
        pltpu.VMEM((layers, slots, width, width), jnp.bfloat16),
        pltpu.VMEM((slots + 1, *block), jnp.int16),
        pltpu.VMEM((24, LANES), jnp.int32),
        pltpu.VMEM((n_peer, 8, LANES), jnp.int32),
        pltpu.SMEM((16, LANES), jnp.int32),
        pltpu.SMEM((n_peer, 8, LANES), jnp.int32),
        *half(nx, ny),
        *half(ny, nx),
        pltpu.VMEM((layers, nz, 4, *block), jnp.int16),
        pltpu.VMEM((layers, nz - 1, 4, *block), jnp.int16),
        pltpu.VMEM((nz, 4, *block), jnp.float32),
        pltpu.SemaphoreType.DMA((layers, n_ag)),
        pltpu.SemaphoreType.DMA((layers, n_ag)),
        pltpu.SemaphoreType.DMA((layers, n_rs)),
        pltpu.SemaphoreType.DMA((layers, n_rs)),
        pltpu.SemaphoreType.DMA((n_peer,)),
        pltpu.SemaphoreType.DMA((n_peer,)),
        pltpu.SemaphoreType.DMA((layers + 2,)),
    ]
    vmem = pl.BlockSpec(memory_space=pltpu.VMEM)
    return pl.pallas_call(
        functools.partial(kernel, sizes, layers, slots, rows),
        out_shape=jax.ShapeDtypeStruct(images.shape, images.dtype),
        in_specs=[
            vmem,
            pl.BlockSpec(memory_space=pltpu.HBM),
            vmem,
            pl.BlockSpec(memory_space=pltpu.SMEM),
            vmem,
        ],
        out_specs=vmem,
        scratch_shapes=scratch,
        compiler_params=pltpu.CompilerParams(
            collective_id=0, has_side_effects=True, vmem_limit_bytes=56 * 1024 * 1024
        ),
        name="layers",
    )(images, tile_weights, turned, counts, bias)


def solution(mesh):
    split = Mesh(
        mesh.devices.reshape(mesh.shape["batch"], 8, 4, 4),
        ("batch", "neuron_0", "neuron_1", "neuron_2"),
    )
    return sharded(split)


def sharded(split):
    sizes = {axis: split.shape[axis] for axis in AXES}
    in_specs = (
        P("batch", AXES),
        P(None, AXES, None, None),
        P(None, AXES, None),
        P(None, AXES),
        P(None, AXES),
    )
    return jax.shard_map(
        functools.partial(local, sizes), mesh=split, in_specs=in_specs,
        out_specs=P("batch", AXES), check_vma=False,
    )
```

time: 310 us -> 104 us (0.34)
  waiting for transfers between devices: 141 us -> 0 us
  Pallas kernels: 0 us -> 102 us
  blocking collectives: 50.8 us -> 0 us
  starting transfers between devices: 44.3 us -> 0 us
  local copies, waits for them, and re-layouts: 41 us -> 1.32 us
  between operations: 13.6 us -> 0.01 us
  matrix products: 9 us -> 0 us
  other arithmetic: 8.36 us -> 0 us
    pallas_call x0 -> x1, Pallas kernels: none -> 102 us  [local(): pl.pallas_call(functools.partial(kernel, sizes, layers, slots, rows), out...]
    all_to_all x4 -> x0, waiting for transfers between devices: 95.1 us -> none  [the longest x2 95.1 us: local(): lax.all_to_all(outgoing, NEURON, split_axis=0, concat_axis=0, tiled=True)]
    all_gather x4 -> x0, blocking collectives: 50.8 us -> none  [gathered_by_axis(): nearer = lax.all_gather(value, axes[-1], axis=dim, tiled=True)]
    all_gather x2 -> x0, waiting for transfers between devices: 46 us -> none  [gathered_by_axis(): nearer = lax.all_gather(value, axes[-1], axis=dim, tiled=True)]
    all_to_all x4 -> x0, starting transfers between devices: 44.2 us -> none  [the longest x2 23.7 us: local(): lax.all_to_all(outgoing, NEURON, split_axis=0, concat_axis=0, tiled=True)]
    scatter x4 -> x0, local copies, waits for them, and re-layouts: 29.1 us -> none  [the longest x2 27.1 us: local(): outgoing = jnp.zeros((devices * capacity, image_rows, block_width), jnp.f...]
    dot_general x4 -> x0, matrix products: 9 us -> none  [the longest x2 6.35 us: local(): jnp.einsum('bsk,skn->sbn', picked, tile_weights[layer_index], preferred_e...]
    reshape x2 -> x0, local copies, waits for them, and re-layouts: 3.9 us -> none  [local(): block_view = whole_acts.reshape(image_rows, all_blocks, block_width)]
  transfers between devices with their start and end apart: 6 -> 0, of which waited for: 4 -> 0; matrix products, arithmetic and copies ran while one was open for 17% -> 0% of each run, Pallas kernels for 0% -> 0%
where the time goes in v1:
time: 104 us; the launch traced here: 103 us
  Pallas kernels  102 us (98%)
  local copies, waits for them, and re-layouts  1.32 us (1%)
    pallas_call x1, Pallas kernels, local(): pl.pallas_call(functools.partial(kernel, sizes, layers, slots, rows), out...  102 us

profile of v1, /device:TPU:32, one launch (start us, length us, event | category | flops | bytes accessed | tf_op | source)
XLA Modules:
  0.0 103.5 jit_solution(12313889388106553286)
XLA Ops:
  0.0 102.2 %layers.1 = bf16[16,512]{1,0:T(8,128)(2,1)} custom-call(bf16[16,512]{1,0:T(8,128)(2,1)} %images.1, bf16[2,128,128,128]{3,2,1,0:T(8,128)(2,1)} %weights.1, s32[2,2,128]{2,1,0:T(2,128)} %bitcast.2, s32[1,2]{1,0:T(1,128)} %bitcast.3, f32[2,512]{1,0:T(2,128)} %bias.1), custom_call_target="tpu_custom_call" | custom-call | tf_op jit(solution)/shard_map/layers/pallas_call | solution.py:426
  102.2 1.3 %copy.7 = bf16[16,512]{1,0:T(8,128)(2,1)} copy(bf16[16,512]{1,0:T(8,128)(2,1)} %layers.1) | data formatting | bytes 32768

commit v2 on v1

v2 whole, which is shorter than its diff:
```python
import functools

import jax
import jax.numpy as jnp
from jax import lax
from jax.experimental import pallas as pl
from jax.experimental.pallas import tpu as pltpu
from jax.sharding import Mesh
from jax.sharding import PartitionSpec as P

AXES = ("neuron_0", "neuron_1", "neuron_2")
Z, Y, X = AXES
CEILING = 32.0
WEIGHT_TOP = 0.375
MESH = pl.DeviceIdType.MESH
LANES = 128


def spot_a(sizes, z, y, x):
    return ((z * sizes[Y] + y) * sizes[X] + x) * 2


def spot_b(sizes, axis, me_z, outer, middle, z):
    total = sizes[Z] * sizes[Y] * sizes[X]
    other = Y if axis == X else X
    base = (2 if axis == X else 3) * total
    turned = (z - me_z + 2 + sizes[Z]) & (sizes[Z] - 1)
    return base + (outer * sizes[other] + middle) * sizes[Z] + turned


def encode(value, scale):
    coded = value * lax.rsqrt(jnp.abs(value) + 1e-30) * scale
    return jnp.round(coded).astype(jnp.int32).astype(jnp.int16)


def decode(coded):
    value = coded.astype(jnp.int32).astype(jnp.float32)
    return value * jnp.abs(value)


def kernel(sizes, layers, slots, rows, images, weights, blocks, count, bias, out, *scratch):
    (acts, held, products, table, peer, stab, speer, x_out, x_in, x_late, x_out2, x_in2, x_own,
     y_out, y_in, y_late, y_out2, y_in2, y_own, z_out, z_in, z_own,
     row_sem, z_sem, near_sem, mid_sem, last_sem, send_sem, first_sem, second_sem, third_sem,
     copy_sem) = scratch
    nz, ny, nx = sizes[Z], sizes[Y], sizes[X]
    me = {axis: lax.axis_index(axis) for axis in AXES}
    zh = nz // 2
    width = rows * 0 + LANES
    shift_x, shift_y = nx.bit_length() - 1, ny.bit_length() - 1
    total = nz * ny * nx
    top = WEIGHT_TOP * CEILING * width
    scale1 = 32700.0 / top ** 0.5
    scale2 = 32700.0 / (top * max(nx, ny)) ** 0.5
    scale3 = 32700.0 / (top * nx * ny) ** 0.5
    back1, back2, back3 = 1 / scale1**2, 1 / scale2**2, 1 / scale3**2

    def other(axis, step):
        return lax.rem(me[axis] + step + sizes[axis], sizes[axis])

    barrier = pltpu.get_barrier_semaphore()
    partners = [{Y: p, X: q} for p in range(ny) for q in range(nx) if p or q]
    partners += [{Z: o} for o in range(1, nz)]
    for steps in partners:
        pl.semaphore_signal(
            barrier, inc=1,
            device_id={axis: other(axis, o) for axis, o in steps.items()}, device_id_type=MESH,
        )

    weight_copies = [
        pltpu.make_async_copy(weights.at[l], held.at[l], copy_sem.at[l]) for l in range(layers)
    ]
    for copy in weight_copies:
        copy.start()

    own_spot = [
        spot_a(sizes, me[Z], me[Y], me[X]),
        spot_a(sizes, me[Z], me[Y], me[X]) + 1,
        spot_b(sizes, X, me[Z], me[X], me[Y], me[Z]),
        spot_b(sizes, Y, me[Z], me[Y], me[X], me[Z]),
    ]

    def put_acts(layer, j, value):
        acts[layer, own_spot[j]] = value

    for j in range(4):
        put_acts(0, j, images[:, j * LANES : (j + 1) * LANES])

    lane = lax.broadcasted_iota(jnp.int32, (1, LANES), 1)
    slot = lax.broadcasted_iota(jnp.int32, (LANES, LANES), 0)
    flat = jnp.concatenate(
        [blocks[0], blocks[1], jnp.zeros((4, LANES), jnp.int32)], axis=0
    )
    upright = jnp.transpose(flat)
    dx = lane & (nx - 1)
    dy = (lane >> shift_x) & (ny - 1)
    dz = lane >> (shift_x + shift_y)
    second = jnp.where((dz & 1) == 0, dy, dx)
    groups = 2 if zh > 1 else 1
    zg = zh // groups
    most = jnp.where((dz & 1) == 0, ny, nx) * zg
    place = (second * zg + (dz >> 1) % zg) * 2
    blank = most * 2
    for l in range(layers):
        r = blocks[l, 0:1, :]
        j = r & 3
        rx = (r >> 2) & (nx - 1)
        ry = (r >> (2 + shift_x)) & (ny - 1)
        rz = r >> (2 + shift_x + shift_y)
        spot = jnp.where(
            j < 2,
            spot_a(sizes, rz, ry, rx) + j,
            jnp.where(
                j == 2,
                spot_b(sizes, X, me[Z], rx, ry, rz),
                spot_b(sizes, Y, me[Z], ry, rx, rz),
            ),
        )
        table[l : l + 1, :] = spot
        key = jnp.where(slot < count[0, l], slot + 1, 0)
        col = upright[:, 2 * l + 1 : 2 * l + 2]
        before = jnp.zeros((1, LANES), jnp.int32)
        ranked = [jnp.zeros((1, LANES), jnp.int32) for _ in range(2)]
        for j in range(4):
            found = jnp.sum(jnp.where(col == lane * 4 + j, key, 0), axis=0, keepdims=True)
            live = found > 0
            table[8 + 4 * l + j : 9 + 4 * l + j, :] = jnp.where(live, found - 1, slots)
            table[16 + 4 * l + j : 17 + 4 * l + j, :] = jnp.where(live, place + before, blank)
            for k in range(2):
                ranked[k] = ranked[k] + jnp.where(before == k, found, 0)
            before = before + live.astype(jnp.int32)
        for k in range(2):
            table[2 + 2 * l + k : 3 + 2 * l + k, :] = jnp.where(
                ranked[k] > 0, ranked[k] - 1, slots
            )
    own_table = pltpu.make_async_copy(table.at[pl.ds(0, 16)], stab, copy_sem.at[layers])
    own_table.start()

    nothing = jnp.zeros((rows, LANES), jnp.int16)
    products[slots] = nothing
    for buffer in (x_in, x_late, y_in, y_late):
        for l in range(layers):
            for o in range(buffer.shape[1]):
                buffer[l, o, buffer.shape[2] - 1] = nothing

    pl.semaphore_wait(barrier, len(partners))

    def remote(src, dst, send, recv, steps):
        return pltpu.make_async_remote_copy(
            src_ref=src, dst_ref=dst, send_sem=send, recv_sem=recv,
            device_id={axis: other(axis, step) for axis, step in steps.items()},
            device_id_type=MESH,
        )

    def send(src, dst, send, recv, steps):
        remote(src, dst, send, recv, steps).start()

    def arrive(ref, recv):
        pltpu.make_async_copy(ref, ref, recv).wait()

    def gather(layer):
        def view(first, size):
            return acts.at[layer, pl.ds(first, size)]

        def share(first, size, recv, steps):
            send(view(first, size), view(first, size), send_sem.at[0], recv, steps)

        rows_by_distance = [0]
        for o in range(1, ny // 2 + 1):
            rows_by_distance += [o] if 2 * o == ny else [o, ny - o]
        for rel in rows_by_distance:
            for o in range(nx):
                if rel or o:
                    steps = {Y: rel, X: o} if rel else {X: o}
                    share(own_spot[0], 2, row_sem.at[rel], steps)
        near = min(5, nz)
        for axis, at in ((X, 2), (Y, 3)):
            for o in sorted(range(1, nz), key=lambda o: min(o, nz - o)):
                turned = (nz - o + 2) % nz
                base = own_spot[at] - (2 % nz)
                group = 0 if turned < near else 1
                send(
                    view(own_spot[at], 1), view(base + turned, 1), send_sem.at[0],
                    near_sem.at[2 * (at - 2) + group], {Z: o},
                )

        half = ny // 2
        tops = nz // 2

        def z_index(step, rel, way):
            if step > tops:
                return None
            if 2 * step == nz and (rows_by_distance.index(rel) % 2 == 0) != (way == 1):
                return None
            return ((step - 1) * ny + rel) * 2 + (way < 0)

        def z_view(far, rel, way):
            return spot_a(sizes, other(Z, -way * far), other(Y, -rel), 0)

        def z_go(step, rel, way):
            n = z_index(step, rel, way)
            if n is not None:
                share(z_view(step - 1, rel, way), 2 * nx, z_sem.at[n], {Z: way})

        def z_come(step, rel, way):
            n = z_index(step, rel, way)
            if n is not None:
                arrive(view(z_view(step, rel, way), 2 * nx), z_sem.at[n])
                z_go(step + 1, rel, way)

        def row(rel):
            units = nx if rel else nx - 1
            arrive(view(spot_a(sizes, me[Z], other(Y, -rel), 0), 2 * units), row_sem.at[rel])
            for way in (1, -1):
                z_go(1, rel, way)

        spans = [(0, near)] + ([(near, nz - near)] if nz > near else [])

        def chunk(axis, middle, group):
            first, size = spans[group]
            other_axis = Y if axis == X else X
            total = nz * ny * nx
            base = (2 if axis == X else 3) * total
            return base + (me[axis] * sizes[other_axis] + middle) * nz + first, size

        def last(axis, rel, group):
            other_axis = Y if axis == X else X
            first, size = chunk(axis, other(other_axis, -rel), group)
            for o in range(1, sizes[axis]):
                share(first, size, last_sem.at[int(axis == Y)], {axis: o})

        def lines(axis, group):
            at = 0 if axis == X else 1
            other_axis = Y if axis == X else X
            first, size = chunk(axis, me[other_axis], group)
            came = size - 1 if group == 0 else size
            if came:
                arrive(view(first, came), near_sem.at[2 * at + group])
            for o in range(1, sizes[other_axis]):
                share(first, size, mid_sem.at[mid(at, group, o)], {other_axis: o})
            last(axis, 0, group)

        def mid(at, group, o):
            return (at * 2 + group) * (max(nx, ny) - 1) + o - 1

        def middle(axis, group, o):
            at = 0 if axis == X else 1
            other_axis = Y if axis == X else X
            first, size = chunk(axis, other(other_axis, -o), group)
            arrive(view(first, size), mid_sem.at[mid(at, group, o)])
            last(axis, o, group)

        both = ((X, ny), (Y, nx))
        row(0)
        for axis, _ in both:
            lines(axis, 0)
        for rel in rows_by_distance[1:]:
            row(rel)
        if len(spans) > 1:
            for axis, _ in both:
                lines(axis, 1)
        steps = [(step, rel) for step in range(1, tops + 1) for rel in rows_by_distance]
        jobs = [
            (axis, group, o)
            for group in range(len(spans))
            for o in range(1, max(nx, ny))
            for axis, n in both
            if o < n
        ]
        for at, (step, rel) in enumerate(steps):
            for way in (1, -1):
                z_come(step, rel, way)
            if at >= 1:
                for job in jobs[:2]:
                    middle(*job)
                jobs = jobs[2:]
        for job in jobs:
            middle(*job)
        for axis, n in both:
            total = nz * ny * nx
            base = (2 if axis == X else 3) * total
            arrive(view(base, total - total // sizes[axis]), last_sem.at[int(axis == Y)])

    sets = [
        (0, X, Y, x_out, (x_in, x_late), x_out2, x_in2, x_own),
        (1, Y, X, y_out, (y_in, y_late), y_out2, y_in2, y_own),
    ]
    n_peer = [0, nx - 1]
    for par, a1, *_ in sets:
        for o in range(1, sizes[a1]):
            n = n_peer[par] + o - 1
            send(table.at[pl.ds(16, 8)], peer.at[n], send_sem.at[1], copy_sem.at[layers + 2], {a1: o})
    all_peers = n_peer[1] + ny - 1

    def device_of(par, zi, c1, c2):
        y, x = (c2, c1) if par == 0 else (c1, c2)
        return ((2 * zi + par) * ny + y) * nx + x

    def loop(length, body, unroll):
        unroll = min(unroll, length)

        @pl.loop(0, length // unroll)
        def _(at):
            for u in range(unroll):
                body(at * unroll + u)

    for layer in range(layers):
        gather(layer)
        if layer == 0:
            own_table.wait()
            arrive(peer, copy_sem.at[layers + 2])
            arrive(peer, send_sem.at[1])
            peer_table = pltpu.make_async_copy(peer, speer, copy_sem.at[layers + 1])
            peer_table.start()
        weight_copies[layer].wait()

        def multiply(s):
            got = jnp.dot(
                acts[layer, stab[layer, s]], held[layer, s], preferred_element_type=jnp.float32
            )
            products[s] = encode(got, scale1)

        loop(slots, multiply, 16)
        if layer == 0:
            peer_table.wait()

        tops = max(nx, ny)

        def first_at(par, group, o):
            return first_sem.at[(par * groups + group) * (tops - 1) + o - 1]

        def second_at(par, group, o):
            return second_sem.at[(par * groups + group) * (tops - 1) + o - 1]

        for group in range(groups):
            for o in range(1, tops):
                for par, a1, a2, out1, in1, *_ in sets:
                    if o >= sizes[a1]:
                        continue
                    target = other(a1, o)
                    span = sizes[a2] * zg * 2

                    def pack(p):
                        q = p >> 1
                        d = device_of(par, group * zg + q % zg, target, q // zg)
                        out1[layer, o - 1, group * span + p] = products[
                            stab[2 + 2 * layer + (p & 1), d]
                        ]

                    loop(span, pack, 8)
                    send(
                        out1.at[layer, o - 1, pl.ds(group * span, span)],
                        in1[group].at[layer, o - 1, pl.ds(0, span)],
                        send_sem.at[2 + par], first_at(par, group, o), {a1: o},
                    )

        for group in range(groups):
            for par, a1, a2, out1, in1, out2, in2, own in sets:
                n1, n2 = sizes[a1], sizes[a2]
                span = n2 * zg * 2
                for o in range(1, n1):
                    arrive(in1[group].at[layer, o - 1, pl.ds(0, span)], first_at(par, group, o))
                for o2 in list(range(1, n2)) + [0]:
                    target = other(a2, o2)

                    def add(at):
                        q = group * zg * 4 + at
                        j = q & 3
                        d = device_of(par, q >> 2, me[a1], target)
                        acc = decode(products[stab[8 + 4 * layer + j, d]])
                        for o in range(1, n1):
                            n = n_peer[par] + o - 1
                            acc = acc + decode(in1[group][layer, o - 1, speer[n, 4 * layer + j, d]])
                        acc = acc * back1
                        if o2:
                            out2[layer, o2 - 1, q] = encode(acc, scale2)
                        else:
                            own[q] = acc

                    loop(zg * 4, add, 4)
                    if o2:
                        part = pl.ds(group * zg * 4, zg * 4)
                        send(
                            out2.at[layer, o2 - 1, part], in2.at[layer, o2 - 1, part],
                            send_sem.at[4 + par], second_at(par, group, o2), {a2: o2},
                        )

        for group in range(groups):
            for par, a1, a2, out1, in1, out2, in2, own in sets:
                n2 = sizes[a2]
                for o in range(1, n2):
                    arrive(
                        in2.at[layer, o - 1, pl.ds(group * zg * 4, zg * 4)],
                        second_at(par, group, o),
                    )

                def add(at):
                    q = group * zg * 4 + at
                    acc = decode(in2[layer, 0, q])
                    for o in range(2, n2):
                        acc = acc + decode(in2[layer, o - 1, q])
                    acc = acc * back2 + own[q]
                    zt = 2 * (q >> 2) + par
                    z_out[layer, zt, q & 3] = encode(acc, scale3)
                    z_own[zt, q & 3] = acc

                loop(zg * 4, add, 4)
                for zi in range(group * zg, group * zg + zg):
                    zt = 2 * zi + par

                    @pl.when(me[Z] != zt)
                    def _():
                        pltpu.make_async_remote_copy(
                            src_ref=z_out.at[layer, zt], dst_ref=z_in.at[layer, me[Z]],
                            send_sem=send_sem.at[6], recv_sem=third_sem.at[0],
                            device_id={Z: zt}, device_id_type=MESH,
                        ).start()

        arrive(z_in.at[layer, pl.ds(0, nz - 1)], third_sem.at[0])
        for j in range(4):
            acc = decode(z_in[layer, other(Z, 1), j])
            for o in range(2, nz):
                acc = acc + decode(z_in[layer, other(Z, o), j])
            acc = acc * back3 + z_own[me[Z], j]
            acc = acc + bias[layer : layer + 1, j * LANES : (j + 1) * LANES]
            done = jnp.clip(acc, 0.0, CEILING).astype(jnp.bfloat16)
            if layer + 1 < layers:
                put_acts(layer + 1, j, done)
            else:
                out[:, j * LANES : (j + 1) * LANES] = done

        arrive(acts.at[layer, pl.ds(0, total * 4 - 4)], send_sem.at[0])
        for par, a1, a2, out1, in1, out2, *_ in sets:
            arrive(out1.at[layer], send_sem.at[2 + par])
            arrive(out2.at[layer], send_sem.at[4 + par])
        arrive(z_out.at[layer, pl.ds(0, nz - 1)], send_sem.at[6])


def local(sizes, images, tile_weights, tile_blocks, tile_count, bias):
    layers, slots, width, _ = tile_weights.shape
    rows = images.shape[0]
    nz, ny, nx = sizes[Z], sizes[Y], sizes[X]
    total = nz * ny * nx
    zh = nz // 2
    turned = jnp.transpose(tile_blocks, (0, 2, 1))
    if slots < LANES:
        turned = jnp.pad(turned, ((0, 0), (0, 0), (0, LANES - slots)), constant_values=0)
    counts = jnp.transpose(tile_count, (1, 0))
    block = (rows, LANES)
    groups = 2 if zh > 1 else 1
    zg = zh // groups
    per_set = groups * (max(nx, ny) - 1)
    n_peer = nx - 1 + ny - 1

    def half(n1, n2):
        return [
            pltpu.VMEM((layers, n1 - 1, n2 * zh * 2, *block), jnp.int16),
            pltpu.VMEM((layers, n1 - 1, n2 * zg * 2 + 1, *block), jnp.int16),
            pltpu.VMEM((layers, n1 - 1, n2 * zg * 2 + 1, *block), jnp.int16),
            pltpu.VMEM((layers, n2 - 1, zh * 4, *block), jnp.int16),
            pltpu.VMEM((layers, n2 - 1, zh * 4, *block), jnp.int16),
            pltpu.VMEM((zh * 4, *block), jnp.float32),
        ]

    scratch = [
        pltpu.VMEM((layers, total * 4, *block), jnp.bfloat16),
        pltpu.VMEM((layers, slots, width, width), jnp.bfloat16),
        pltpu.VMEM((slots + 1, *block), jnp.int16),
        pltpu.VMEM((24, LANES), jnp.int32),
        pltpu.VMEM((n_peer, 8, LANES), jnp.int32),
        pltpu.SMEM((16, LANES), jnp.int32),
        pltpu.SMEM((n_peer, 8, LANES), jnp.int32),
        *half(nx, ny),
        *half(ny, nx),
        pltpu.VMEM((layers, nz, 4, *block), jnp.int16),
        pltpu.VMEM((layers, nz, 4, *block), jnp.int16),
        pltpu.VMEM((nz, 4, *block), jnp.float32),
        pltpu.SemaphoreType.DMA((ny,)),
        pltpu.SemaphoreType.DMA((nz // 2 * ny * 2,)),
        pltpu.SemaphoreType.DMA((4,)),
        pltpu.SemaphoreType.DMA((4 * (max(nx, ny) - 1),)),
        pltpu.SemaphoreType.DMA((2,)),
        pltpu.SemaphoreType.DMA((7,)),
        pltpu.SemaphoreType.DMA((2 * per_set,)),
        pltpu.SemaphoreType.DMA((2 * per_set,)),
        pltpu.SemaphoreType.DMA((1,)),
        pltpu.SemaphoreType.DMA((layers + 3,)),
    ]
    vmem = pl.BlockSpec(memory_space=pltpu.VMEM)
    return pl.pallas_call(
        functools.partial(kernel, sizes, layers, slots, rows),
        out_shape=jax.ShapeDtypeStruct(images.shape, images.dtype),
        in_specs=[
            vmem,
            pl.BlockSpec(memory_space=pltpu.HBM),
            vmem,
            pl.BlockSpec(memory_space=pltpu.SMEM),
            vmem,
        ],
        out_specs=vmem,
        scratch_shapes=scratch,
        compiler_params=pltpu.CompilerParams(
            collective_id=0, has_side_effects=True, vmem_limit_bytes=56 * 1024 * 1024
        ),
        name="layers",
    )(images, tile_weights, turned, counts, bias)


def solution(mesh):
    split = Mesh(
        mesh.devices.reshape(mesh.shape["batch"], 8, 4, 4),
        ("batch", "neuron_0", "neuron_1", "neuron_2"),
    )
    return sharded(split)


def sharded(split):
    sizes = {axis: split.shape[axis] for axis in AXES}
    in_specs = (
        P("batch", AXES),
        P(None, AXES, None, None),
        P(None, AXES, None),
        P(None, AXES),
        P(None, AXES),
    )
    return jax.shard_map(
        functools.partial(local, sizes), mesh=split, in_specs=in_specs,
        out_specs=P("batch", AXES), check_vma=False,
    )
```

time: 104 us -> 88 us (0.85)
  Pallas kernels: 102 us -> 86.4 us
    pallas_call x1, Pallas kernels: 102 us -> 86.4 us  [local(): pl.pallas_call(functools.partial(kernel, sizes, layers, slots, rows), out...]
where the time goes in v2:
time: 88 us; the launch traced here: 87.7 us
  Pallas kernels  86.4 us (98%)
  local copies, waits for them, and re-layouts  1.32 us (2%)
    pallas_call x1, Pallas kernels, local(): pl.pallas_call(functools.partial(kernel, sizes, layers, slots, rows), out...  86.4 us

profile of v2, /device:TPU:32, one launch (start us, length us, event | category | flops | bytes accessed | tf_op | source)
XLA Modules:
  0.0 87.7 jit_solution(4951387360558881118)
XLA Ops:
  0.0 86.4 %layers.1 = bf16[16,512]{1,0:T(8,128)(2,1)} custom-call(bf16[16,512]{1,0:T(8,128)(2,1)} %images.1, bf16[2,128,128,128]{3,2,1,0:T(8,128)(2,1)} %weights.1, s32[2,2,128]{2,1,0:T(2,128)} %bitcast.2, s32[1,2]{1,0:T(1,128)} %bitcast.3, f32[2,512]{1,0:T(2,128)} %bias.1), custom_call_target="tpu_custom_call" | custom-call | tf_op jit(solution)/shard_map/layers/pallas_call | solution.py:490
  86.4 1.3 %copy.7 = bf16[16,512]{1,0:T(8,128)(2,1)} copy(bf16[16,512]{1,0:T(8,128)(2,1)} %layers.1) | data formatting | bytes 32768

commit v3 on v2

--- a/solution.py
+++ b/solution.py
@@ -16,16 +16,33 @@
 LANES = 128
 
 
-def spot_a(sizes, z, y, x):
-    return ((z * sizes[Y] + y) * sizes[X] + x) * 2
-
-
-def spot_b(sizes, axis, me_z, outer, middle, z):
-    total = sizes[Z] * sizes[Y] * sizes[X]
+SHARES = ((1, 2, 1), (1, 1, 2))
+
+
+def spot_a(sizes, shares, z, y, x):
+    return ((z * sizes[Y] + y) * sizes[X] + x) * shares[0]
+
+
+def base_of(sizes, shares, axis):
+    return sizes[Z] * sizes[Y] * sizes[X] * (shares[0] + (shares[1] if axis == Y else 0))
+
+
+def share_of(shares, axis):
+    return shares[1] if axis == X else shares[2]
+
+
+def spot_b(sizes, shares, axis, me_z, outer, middle, z):
     other = Y if axis == X else X
-    base = (2 if axis == X else 3) * total
     turned = (z - me_z + 2 + sizes[Z]) & (sizes[Z] - 1)
-    return base + (outer * sizes[other] + middle) * sizes[Z] + turned
+    spot = (outer * sizes[other] + middle) * sizes[Z] + turned
+    return base_of(sizes, shares, axis) + spot * share_of(shares, axis)
+
+
+GROUPS = 4
+
+
+def groups_of(zh):
+    return min(GROUPS, zh)
 
 
 def encode(value, scale):
@@ -39,17 +56,19 @@
 
 
 def kernel(sizes, layers, slots, rows, images, weights, blocks, count, bias, out, *scratch):
-    (acts, held, products, table, peer, stab, speer, x_out, x_in, x_late, x_out2, x_in2, x_own,
-     y_out, y_in, y_late, y_out2, y_in2, y_own, z_out, z_in, z_own,
+    (acts, held, products, table, peer, stab, speer, x_out, x_out2, x_in2, x_own,
+     y_out, y_out2, y_in2, y_own, z_out, z_in, z_own,
      row_sem, z_sem, near_sem, mid_sem, last_sem, send_sem, first_sem, second_sem, third_sem,
-     copy_sem) = scratch
+     copy_sem, *late) = scratch
     nz, ny, nx = sizes[Z], sizes[Y], sizes[X]
     me = {axis: lax.axis_index(axis) for axis in AXES}
     zh = nz // 2
-    width = rows * 0 + LANES
+    groups = groups_of(zh)
+    zg = zh // groups
+    x_in, y_in = late[:groups], late[groups:]
     shift_x, shift_y = nx.bit_length() - 1, ny.bit_length() - 1
     total = nz * ny * nx
-    top = WEIGHT_TOP * CEILING * width
+    top = WEIGHT_TOP * CEILING * LANES
     scale1 = 32700.0 / top ** 0.5
     scale2 = 32700.0 / (top * max(nx, ny)) ** 0.5
     scale3 = 32700.0 / (top * nx * ny) ** 0.5
@@ -73,12 +92,20 @@
     for copy in weight_copies:
         copy.start()
 
-    own_spot = [
-        spot_a(sizes, me[Z], me[Y], me[X]),
-        spot_a(sizes, me[Z], me[Y], me[X]) + 1,
-        spot_b(sizes, X, me[Z], me[X], me[Y], me[Z]),
-        spot_b(sizes, Y, me[Z], me[Y], me[X], me[Z]),
-    ]
+    core = lax.axis_index("batch")
+
+    def own_spots(shares):
+        first_a = spot_a(sizes, shares, me[Z], me[Y], me[X])
+        first_b = spot_b(sizes, shares, X, me[Z], me[X], me[Y], me[Z])
+        first_c = spot_b(sizes, shares, Y, me[Z], me[Y], me[X], me[Z])
+        return [
+            first + at
+            for first, share in zip((first_a, first_b, first_c), shares)
+            for at in range(share)
+        ]
+
+    both_spots = [own_spots(shares) for shares in SHARES]
+    own_spot = [p + core * (q - p) for p, q in zip(*both_spots)]
 
     def put_acts(layer, j, value):
         acts[layer, own_spot[j]] = value
@@ -96,8 +123,6 @@
     dy = (lane >> shift_x) & (ny - 1)
     dz = lane >> (shift_x + shift_y)
     second = jnp.where((dz & 1) == 0, dy, dx)
-    groups = 2 if zh > 1 else 1
-    zg = zh // groups
     most = jnp.where((dz & 1) == 0, ny, nx) * zg
     place = (second * zg + (dz >> 1) % zg) * 2
     blank = most * 2
@@ -107,15 +132,18 @@
         rx = (r >> 2) & (nx - 1)
         ry = (r >> (2 + shift_x)) & (ny - 1)
         rz = r >> (2 + shift_x + shift_y)
-        spot = jnp.where(
-            j < 2,
-            spot_a(sizes, rz, ry, rx) + j,
-            jnp.where(
-                j == 2,
-                spot_b(sizes, X, me[Z], rx, ry, rz),
-                spot_b(sizes, Y, me[Z], ry, rx, rz),
-            ),
-        )
+        spots = []
+        for shares in SHARES:
+            in_a, in_b, in_c = (
+                spot_a(sizes, shares, rz, ry, rx),
+                spot_b(sizes, shares, X, me[Z], rx, ry, rz),
+                spot_b(sizes, shares, Y, me[Z], ry, rx, rz),
+            )
+            to_b, to_c = shares[0], shares[0] + shares[1]
+            spots.append(
+                jnp.where(j < to_b, in_a + j, jnp.where(j < to_c, in_b + j - to_b, in_c + j - to_c))
+            )
+        spot = spots[0] + core * (spots[1] - spots[0])
         table[l : l + 1, :] = spot
         key = jnp.where(slot < count[0, l], slot + 1, 0)
         col = upright[:, 2 * l + 1 : 2 * l + 2]
@@ -138,7 +166,7 @@
 
     nothing = jnp.zeros((rows, LANES), jnp.int16)
     products[slots] = nothing
-    for buffer in (x_in, x_late, y_in, y_late):
+    for buffer in late:
         for l in range(layers):
             for o in range(buffer.shape[1]):
                 buffer[l, o, buffer.shape[2] - 1] = nothing
@@ -158,7 +186,10 @@
     def arrive(ref, recv):
         pltpu.make_async_copy(ref, ref, recv).wait()
 
-    def gather(layer):
+    def gather(layer, shares):
+        own = own_spots(shares)
+        starts = (own[0], own[shares[0]], own[shares[0] + shares[1]])
+
         def view(first, size):
             return acts.at[layer, pl.ds(first, size)]
 
@@ -172,16 +203,17 @@
             for o in range(nx):
                 if rel or o:
                     steps = {Y: rel, X: o} if rel else {X: o}
-                    share(own_spot[0], 2, row_sem.at[rel], steps)
+                    share(starts[0], shares[0], row_sem.at[rel], steps)
         near = min(5, nz)
-        for axis, at in ((X, 2), (Y, 3)):
+        for axis, at in ((X, 0), (Y, 1)):
+            width = share_of(shares, axis)
             for o in sorted(range(1, nz), key=lambda o: min(o, nz - o)):
                 turned = (nz - o + 2) % nz
-                base = own_spot[at] - (2 % nz)
+                base = starts[1 + at] - (2 % nz) * width
                 group = 0 if turned < near else 1
                 send(
-                    view(own_spot[at], 1), view(base + turned, 1), send_sem.at[0],
-                    near_sem.at[2 * (at - 2) + group], {Z: o},
+                    view(starts[1 + at], width), view(base + turned * width, width),
+                    send_sem.at[0], near_sem.at[2 * at + group], {Z: o},
                 )
 
         half = ny // 2
@@ -195,22 +227,23 @@
             return ((step - 1) * ny + rel) * 2 + (way < 0)
 
         def z_view(far, rel, way):
-            return spot_a(sizes, other(Z, -way * far), other(Y, -rel), 0)
+            return spot_a(sizes, shares, other(Z, -way * far), other(Y, -rel), 0)
 
         def z_go(step, rel, way):
             n = z_index(step, rel, way)
             if n is not None:
-                share(z_view(step - 1, rel, way), 2 * nx, z_sem.at[n], {Z: way})
+                share(z_view(step - 1, rel, way), shares[0] * nx, z_sem.at[n], {Z: way})
 
         def z_come(step, rel, way):
             n = z_index(step, rel, way)
             if n is not None:
-                arrive(view(z_view(step, rel, way), 2 * nx), z_sem.at[n])
+                arrive(view(z_view(step, rel, way), shares[0] * nx), z_sem.at[n])
                 z_go(step + 1, rel, way)
 
         def row(rel):
             units = nx if rel else nx - 1
-            arrive(view(spot_a(sizes, me[Z], other(Y, -rel), 0), 2 * units), row_sem.at[rel])
+            first = spot_a(sizes, shares, me[Z], other(Y, -rel), 0)
+            arrive(view(first, shares[0] * units), row_sem.at[rel])
             for way in (1, -1):
                 z_go(1, rel, way)
 
@@ -219,9 +252,9 @@
         def chunk(axis, middle, group):
             first, size = spans[group]
             other_axis = Y if axis == X else X
-            total = nz * ny * nx
-            base = (2 if axis == X else 3) * total
-            return base + (me[axis] * sizes[other_axis] + middle) * nz + first, size
+            width = share_of(shares, axis)
+            spot = (me[axis] * sizes[other_axis] + middle) * nz + first
+            return base_of(sizes, shares, axis) + spot * width, size * width
 
         def last(axis, rel, group):
             other_axis = Y if axis == X else X
@@ -233,7 +266,7 @@
             at = 0 if axis == X else 1
             other_axis = Y if axis == X else X
             first, size = chunk(axis, me[other_axis], group)
-            came = size - 1 if group == 0 else size
+            came = size - share_of(shares, axis) if group == 0 else size
             if came:
                 arrive(view(first, came), near_sem.at[2 * at + group])
             for o in range(1, sizes[other_axis]):
@@ -277,13 +310,12 @@
         for job in jobs:
             middle(*job)
         for axis, n in both:
-            total = nz * ny * nx
-            base = (2 if axis == X else 3) * total
-            arrive(view(base, total - total // sizes[axis]), last_sem.at[int(axis == Y)])
+            came = (total - total // sizes[axis]) * share_of(shares, axis)
+            arrive(view(base_of(sizes, shares, axis), came), last_sem.at[int(axis == Y)])
 
     sets = [
-        (0, X, Y, x_out, (x_in, x_late), x_out2, x_in2, x_own),
-        (1, Y, X, y_out, (y_in, y_late), y_out2, y_in2, y_own),
+        (0, X, Y, x_out, x_in, x_out2, x_in2, x_own),
+        (1, Y, X, y_out, y_in, y_out2, y_in2, y_own),
     ]
     n_peer = [0, nx - 1]
     for par, a1, *_ in sets:
@@ -305,7 +337,12 @@
                 body(at * unroll + u)
 
     for layer in range(layers):
-        gather(layer)
+        for at, shares in enumerate(SHARES):
+
+            @pl.when(core == at)
+            def _(shares=shares):
+                gather(layer, shares)
+
         if layer == 0:
             own_table.wait()
             arrive(peer, copy_sem.at[layers + 2])
@@ -447,7 +484,7 @@
         turned = jnp.pad(turned, ((0, 0), (0, 0), (0, LANES - slots)), constant_values=0)
     counts = jnp.transpose(tile_count, (1, 0))
     block = (rows, LANES)
-    groups = 2 if zh > 1 else 1
+    groups = groups_of(zh)
     zg = zh // groups
     per_set = groups * (max(nx, ny) - 1)
     n_peer = nx - 1 + ny - 1
@@ -455,8 +492,6 @@
     def half(n1, n2):
         return [
             pltpu.VMEM((layers, n1 - 1, n2 * zh * 2, *block), jnp.int16),
-            pltpu.VMEM((layers, n1 - 1, n2 * zg * 2 + 1, *block), jnp.int16),
-            pltpu.VMEM((layers, n1 - 1, n2 * zg * 2 + 1, *block), jnp.int16),
             pltpu.VMEM((layers, n2 - 1, zh * 4, *block), jnp.int16),
             pltpu.VMEM((layers, n2 - 1, zh * 4, *block), jnp.int16),
             pltpu.VMEM((zh * 4, *block), jnp.float32),
@@ -485,6 +520,11 @@
         pltpu.SemaphoreType.DMA((2 * per_set,)),
         pltpu.SemaphoreType.DMA((1,)),
         pltpu.SemaphoreType.DMA((layers + 3,)),
+        *[
+            pltpu.VMEM((layers, n1 - 1, n2 * zg * 2 + 1, *block), jnp.int16)
+            for n1, n2 in ((nx, ny), (ny, nx))
+            for _ in range(groups)
+        ],
     ]
     vmem = pl.BlockSpec(memory_space=pltpu.VMEM)
     return pl.pallas_call(

time: 88 us -> 82.8 us (0.941)
  Pallas kernels: 86.4 us -> 81.3 us
    pallas_call x1, Pallas kernels: 86.4 us -> 81.3 us  [local(): pl.pallas_call(functools.partial(kernel, sizes, layers, slots, rows), out...]
where the time goes in v3:
time: 82.8 us; the launch traced here: 82.6 us
  Pallas kernels  81.3 us (98%)
  local copies, waits for them, and re-layouts  1.32 us (2%)
    pallas_call x1, Pallas kernels, local(): pl.pallas_call(functools.partial(kernel, sizes, layers, slots, rows), out...  81.3 us

profile of v3, /device:TPU:32, one launch (start us, length us, event | category | flops | bytes accessed | tf_op | source)
XLA Modules:
  0.0 82.6 jit_solution(13464327189000870645)
XLA Ops:
  0.0 81.3 %layers.1 = bf16[16,512]{1,0:T(8,128)(2,1)} custom-call(bf16[16,512]{1,0:T(8,128)(2,1)} %images.1, bf16[2,128,128,128]{3,2,1,0:T(8,128)(2,1)} %weights.1, s32[2,2,128]{2,1,0:T(2,128)} %bitcast.2, s32[1,2]{1,0:T(1,128)} %bitcast.3, f32[2,512]{1,0:T(2,128)} %bias.1), custom_call_target="tpu_custom_call" | custom-call | tf_op jit(solution)/shard_map/layers/pallas_call | solution.py:530
  81.3 1.3 %copy.7 = bf16[16,512]{1,0:T(8,128)(2,1)} copy(bf16[16,512]{1,0:T(8,128)(2,1)} %layers.1) | data formatting | bytes 32768
